TPU v7x, 32 devices: a whole 2x2x4 slice. The times are simulated.
32 devices in a mesh: walker: 8 (over z, core), chol: 4 (over y, x).
Axes of the slice: x: 2, y: 2, z: 4, core: 2. Of those that a mesh axis runs over, the one named last changes fastest.
Arguments:
- chol_vectors: bfloat16 [256, 768, 192], P('chol', 'walker'), may hold values from -0.2 to 0.2, as said below
- green: bfloat16 [16, 768, 192], P('walker'), may hold values from -6 to 6
Outputs:
- energy: float32 [16], P('walker')
- gradient: float32 [16, 768, 192], P('walker', 'chol')
Inputs may be any that keep to these rules, and one draw needn't show every extreme that they name: `chol_vectors`: independent entries of each vector; vector magnitudes differ from vector to vector.
All inputs are finite; a program needn't handle non-finite values.
Results may differ from a plain program's by a relative error of at most 0.0042.
Values may be sent and summed in bfloat16 or wider, within the bound.
A program may use at most 128 MiB of HBM per device.

v0:
```python
import functools
import math

import jax
import jax.numpy as jnp
from jax import lax
from jax.experimental import pallas as pl
from jax.experimental.pallas import tpu as pltpu
from jax.sharding import PartitionSpec as P

MESH = pl.DeviceIdType.MESH
CORES = 2
ANY = pl.BlockSpec(memory_space=pl.ANY)


def remote(src, dst, send, recv, device):
    return pltpu.make_async_remote_copy(
        src_ref=src, dst_ref=dst, send_sem=send, recv_sem=recv, device_id=device, device_id_type=MESH
    )


def greet(devices):
    barrier = pltpu.get_barrier_semaphore()
    for device in devices:
        pl.semaphore_signal(barrier, inc=1, device_id=device, device_id_type=MESH)
    pl.semaphore_wait(barrier, len(devices))


def gather_kernel(
    span, groups, chol, green, blocks, greens, own_chol, own_green,
    chol_send, chol_recv, pair_send, pair_recv, green_send, green_recv, share_send, share_recv, local,
):
    walker, group = lax.axis_index("walker"), lax.axis_index("chol")
    chip, core = walker // CORES, walker % CORES
    kept, width = blocks.shape[1], green.shape[1] // groups
    partner = (chip * CORES + 1 - core, group)
    peers = [None] + [lax.rem(chip + d, span) for d in range(1, span)]
    sources = [None] + [lax.rem(chip - d + span, span) for d in range(1, span)]
    sides = [None] + [(walker, lax.rem(group + d, groups)) for d in range(1, groups)]
    greet([partner] + [(z * CORES + core, group) for z in peers[1:]] + sides[1:])

    mine = pl.ds(pl.multiple_of(group * width, math.gcd(width, 16)), width)
    waits = []
    first, quarters = [None], [None]
    for d in range(1, span):
        target = (peers[d] * CORES + core, group)
        quarter = remote(
            green.at[:, mine, :], greens.at[chip, :, mine, :], green_send.at[d], green_recv.at[d], target
        )
        quarter.start()
        quarters.append(quarter)
    for d in range(1, span):
        target = (peers[d] * CORES + core, group)
        block = remote(
            chol.at[pl.ds(peers[d] * kept, kept)], blocks.at[walker], chol_send.at[d], chol_recv.at[d], target
        )
        block.start()
        first.append(block)
    held = chol.at[pl.ds(chip * kept, kept)]
    pair = remote(held, blocks.at[walker], pair_send.at[0], pair_recv.at[0], partner)
    pair.start()
    waits.append(pair)
    takes = [pltpu.make_async_copy(held, own_chol, local.at[0]), pltpu.make_async_copy(green, own_green, local.at[1])]
    for take in takes:
        take.start()
    for take in takes:
        take.wait()
    puts = [
        pltpu.make_async_copy(own_chol, blocks.at[walker], local.at[2]),
        pltpu.make_async_copy(own_green, greens.at[chip], local.at[3]),
    ]
    for put in puts:
        put.start()
    for d in range(1, span):
        quarters[d].wait_recv()
        piece = greens.at[sources[d], :, mine, :]
        for e in range(1, groups):
            share = remote(piece, piece, share_send.at[d, e], share_recv.at[d, e], sides[e])
            share.start()
            waits.append(share)
    for d in range(1, span):
        first[d].wait_recv()
        landed = blocks.at[sources[d] * CORES + core]
        pair = remote(landed, landed, pair_send.at[d], pair_recv.at[d], partner)
        pair.start()
        waits.append(pair)
    for put in puts:
        put.wait()
    for d in range(1, span):
        quarters[d].wait_send()
        first[d].wait_send()
    for copy in waits:
        copy.wait()


def gather(span, groups, chol, green):
    kl, mb, width = chol.shape
    wl, m, _ = green.shape
    kept = kl // span
    dma = pltpu.SemaphoreType.DMA
    return pl.pallas_call(
        functools.partial(gather_kernel, span, groups),
        out_shape=(
            jax.ShapeDtypeStruct((span * CORES, kept, mb, width), chol.dtype),
            jax.ShapeDtypeStruct((span, wl, m, width), green.dtype),
        ),
        in_specs=[ANY, ANY],
        out_specs=(ANY, ANY),
        scratch_shapes=[
            pltpu.VMEM((kept, mb, width), chol.dtype),
            pltpu.VMEM((wl, m, width), green.dtype),
            dma((span,)), dma((span,)), dma((span,)), dma((span,)), dma((span,)), dma((span,)),
            dma((span, groups)), dma((span, groups)), dma((4,)),
        ],
        compiler_params=pltpu.CompilerParams(collective_id=0, has_side_effects=True),
    )(chol, green)


def product_kernel(chol, green, terms, energy, turned, total):
    k = pl.program_id(1)
    walkers = green.shape[0]

    @pl.when(k == 0)
    def _():
        total[...] = jnp.zeros_like(total)
        energy[...] = jnp.zeros_like(energy)

    turned[...] = chol[0].T
    per = math.gcd(walkers, 4)

    def step(n, carry):
        for u in range(per):
            w = n * per + u
            tmat = jnp.dot(turned[...], green[w], preferred_element_type=jnp.float32)
            energy[w] += jnp.sum(tmat * tmat.T, axis=0, keepdims=True)
            total[w] += lax.dot_general(
                chol[0], tmat.astype(jnp.bfloat16), (((1,), (1,)), ((), ())), preferred_element_type=jnp.float32
            )
        return carry

    lax.fori_loop(0, walkers // per, step, 0)

    @pl.when(k == pl.num_programs(1) - 1)
    def _():
        terms[...] = total[...].astype(terms.dtype)


def products(chol, green):
    kept, m, width = chol.shape
    walkers = green.shape[0]
    some = math.gcd(walkers, 8)
    return pl.pallas_call(
        product_kernel,
        out_shape=(
            jax.ShapeDtypeStruct((walkers, m, width), jnp.bfloat16),
            jax.ShapeDtypeStruct((walkers, 1, width), jnp.float32),
        ),
        grid=(walkers // some, kept),
        in_specs=[
            pl.BlockSpec((1, m, width), lambda g, k: (k, 0, 0)),
            pl.BlockSpec((some, m, width), lambda g, k: (g, 0, 0)),
        ],
        out_specs=(
            pl.BlockSpec((some, m, width), lambda g, k: (g, 0, 0)),
            pl.BlockSpec((some, 1, width), lambda g, k: (g, 0, 0)),
        ),
        scratch_shapes=[pltpu.VMEM((width, m), jnp.bfloat16), pltpu.VMEM((some, m, width), jnp.float32)],
        compiler_params=pltpu.CompilerParams(
            dimension_semantics=("arbitrary", "arbitrary"), vmem_limit_bytes=60 * 2**20
        ),
    )(chol, green)


def spread_kernel(span, groups, terms, energy, parts, energies, send, recv, esend, erecv):
    walker, group = lax.axis_index("walker"), lax.axis_index("chol")
    chip, core = walker // CORES, walker % CORES
    wl, width = parts.shape[1], parts.shape[2]
    others = [(d, e) for d in range(span) for e in range(groups) if d + e > 0]
    target = {(d, e): (lax.rem(chip + d, span), lax.rem(group + e, groups)) for d, e in others}
    greet([(target[o][0] * CORES + core, target[o][1]) for o in others])
    copies = []
    for n, o in enumerate(others):
        z, q = target[o]
        device = (z * CORES + core, q)
        block = terms.at[pl.ds(z * wl, wl), pl.ds(pl.multiple_of(q * width, math.gcd(width, 16)), width), :]
        copies.append(remote(block, parts.at[n], send.at[n], recv.at[n], device))
        copies.append(remote(energy.at[z], energies.at[n], esend.at[n], erecv.at[n], device))
    for copy in copies:
        copy.start()
    for copy in copies:
        copy.wait()


def spread(span, groups, terms, energy):
    walkers, m, width = terms.shape
    count = span * groups - 1
    dma = pltpu.SemaphoreType.DMA
    return pl.pallas_call(
        functools.partial(spread_kernel, span, groups),
        out_shape=(
            jax.ShapeDtypeStruct((count, walkers // span, m // groups, width), terms.dtype),
            jax.ShapeDtypeStruct((count,) + energy.shape[1:], energy.dtype),
        ),
        in_specs=[ANY, ANY],
        out_specs=(ANY, ANY),
        scratch_shapes=[dma((count,)), dma((count,)), dma((count,)), dma((count,))],
        compiler_params=pltpu.CompilerParams(collective_id=1, has_side_effects=True),
    )(terms, energy)


def per_device(span, groups, chol_vectors, green):
    kl, mb, width = chol_vectors.shape
    wl, m, _ = green.shape
    nchol = kl * groups
    escale = 1.0 / (nchol * width)
    gscale = 1.0 / nchol**0.5
    chip, group = lax.axis_index("walker") // CORES, lax.axis_index("chol")

    blocks, greens = gather(span, groups, chol_vectors, green)
    chol = jnp.transpose(blocks, (1, 0, 2, 3)).reshape(kl // span, m, width)
    terms, lines = products(chol, greens.reshape(span * wl, m, width))

    sums = jnp.sum(lines, axis=(1, 2)).reshape(span, wl, 1)
    sums = jnp.broadcast_to(sums, (span, wl, 128))
    parts, energies = spread(span, groups, terms, sums)
    own = lax.dynamic_slice(terms, (chip * wl, group * (m // groups), 0), (wl, m // groups, width))
    gradient = (own.astype(jnp.float32) + jnp.sum(parts.astype(jnp.float32), axis=0)) * gscale
    energy = lax.dynamic_index_in_dim(sums, chip, 0, keepdims=False) + jnp.sum(energies, axis=0)
    return energy[:, 0] * escale, gradient


def solution(mesh):
    span, groups = mesh.shape["walker"] // CORES, mesh.shape["chol"]
    return jax.shard_map(
        functools.partial(per_device, span, groups),
        mesh=mesh,
        in_specs=(P("chol", "walker", None), P("walker", None, None)),
        out_specs=(P("walker"), P("walker", "chol", None)),
        check_vma=False,
    )
```

profile of v0, /device:TPU:24, one launch (start us, length us, event | category | flops | bytes accessed | tf_op | source)
XLA Modules:
  0.0 227.7 jit_solution(3528654978375088735)
XLA Ops:
  0.6 2.2 copy.10.green
  2.9 91.9 %shard_map.41 = (bf16[8,16,96,192]{3,2,1,0:T(8,128)(2,1)}, bf16[4,2,768,192]{3,2,1,0:T(8,128)(2,1)}) custom-call(bf16[64,96,192]{2,1,0:T(8,128)(2,1)} %chol.1, bf16[2,768,192]{2,1,0:T(8,128)(2,1)} %copy.10.green), custom_call_target="tpu_custom_call" | custom-call | tf_op jit(solution)/shard_map/pallas_call | solution.py:101
  94.7 6.1 %copy.11 = bf16[16,8,96,192]{3,2,1,0:T(8,128)(2,1)} copy(bf16[16,8,96,192]{3,2,0,1:T(8,128)(2,1)} %bitcast.6) | data formatting | bytes 9437184 | tf_op jit(solution)/shard_map/transpose | solution.py:220
  100.8 43.5 %shard_map.42 = (bf16[8,768,192]{2,1,0:T(8,128)(2,1)}, f32[8,1,192]{2,1,0:T(1,128)}) custom-call(bf16[16,768,192]{2,1,0:T(8,128)(2,1)} %bitcast.5, bf16[8,768,192]{2,1,0:T(8,128)(2,1)} %bitcast.7), custom_call_target="tpu_custom_call" | custom-call | tf_op jit(solution)/shard_map/pallas_call | solution.py:152
  144.3 0.8 reduce_sum.27
  145.1 0.1 broadcast_in_dim.11
  145.2 0.7 broadcast_in_dim.14.energy
  145.9 76.3 %shard_map.43 = (bf16[15,2,192,192]{3,2,1,0:T(8,128)(2,1)}, f32[15,2,128]{2,1,0:T(2,128)}) custom-call(bf16[8,768,192]{2,1,0:T(8,128)(2,1)} %get-tuple-element.11.terms, f32[4,2,128]{2,1,0:T(2,128)} %broadcast_in_dim.14.energy), custom_call_target="tpu_custom_call" | custom-call | tf_op jit(solution)/shard_map/pallas_call | solution.py:198
  222.1 0.7 reduce_sum.28
  222.9 0.1 broadcast_add_fusion
  223.0 0.6 multiply_reduce_fusion
  223.6 2.4 %convert_reduce_fusion = f32[2,192,192]{2,1,0:T(8,128)S(1)} fusion(bf16[15,2,192,192]{3,2,1,0:T(8,128)(2,1)} %get-tuple-element.13), kind=kLoop, calls=%fused_computation | loop fusion | flops 2138112 | bytes 2506752 | tf_op jit(solution)/shard_map/reduce_sum | solution.py:227
  226.0 1.7 add_multiply_fusion
  (1 shorter events, 0.0 us)
where the time goes:
time: 228 us
  Pallas kernels  212 us (93%)
  local copies, waits for them, and re-layouts  9.06 us (4%)
  other arithmetic  6.37 us (3%)
    pallas_call x1, Pallas kernels, gather(): pl.pallas_call(functools.partial(gather_kernel, span, groups), out_shape=...  91.9 us
    pallas_call x1, Pallas kernels, spread(): pl.pallas_call(functools.partial(spread_kernel, span, groups), out_shape=...  76.3 us
    pallas_call x1, Pallas kernels, products(): pl.pallas_call(product_kernel, out_shape=(jax.ShapeDtypeStruct((walkers,...  43.5 us
    transpose x1, local copies, waits for them, and re-layouts, per_device(): chol = jnp.transpose(blocks, (1, 0, 2, 3)).reshape(kl // span, m, width)  6.07 us

commit v1 on v0

--- a/solution.py
+++ b/solution.py
@@ -208,6 +208,379 @@
     )(terms, energy)
 
 
+LANES = 128
+HALF = LANES // 2
+BATCH = 4
+
+
+def flip(index, bits):
+    for b in range(8):
+        if (bits >> b) & 1:
+            step = 1 << b
+            index = index + step - 2 * step * lax.rem(lax.div(index, step), 2)
+    return index
+
+
+def join(left, right):
+    return jnp.concatenate([left, right], axis=1)
+
+
+def fused_kernel(
+    span, groups, gscale, chol, green, out, energy,
+    raw, packed, vectors, own, greens, turned, tmat, mixed, total, outgoing, incoming, last_out, last_in, lines, arrived,
+    local, chol_send, chol_recv, pair_send, pair_recv, green_send, green_recv, share_send, share_recv,
+    grad_send, grad_recv, last_send, last_recv, line_send, line_recv,
+):
+    walker, group = lax.axis_index("walker"), lax.axis_index("chol")
+    chip, core = lax.div(walker, CORES), lax.rem(walker, CORES)
+    kept, mb = raw.shape[1], raw.shape[2]
+    m = total.shape[1]
+    chunks = kept // BATCH
+    quarter = m // groups
+    part = quarter // 2
+    cell = 3 * LANES
+    bits = [1 << b for b in range(groups.bit_length() - 1)]
+    orders = [bits, bits[::-1]]
+    partner = (chip * CORES + 1 - core, group)
+
+    def device(r, e):
+        return (flip(chip, r) * CORES + core, flip(group, e))
+
+    others = [(r, e) for r in range(span) for e in range(groups) if r + e > 0]
+    barrier = pltpu.get_barrier_semaphore()
+    for peer in [partner] + [device(r, e) for r, e in others]:
+        pl.semaphore_signal(barrier, inc=1, device_id=peer, device_id_type=MESH)
+
+    loads = [
+        pltpu.make_async_copy(chol.at[pl.ds(flip(chip, r) * kept, kept)], raw.at[r], local.at[r]) for r in range(span)
+    ]
+    load_green = pltpu.make_async_copy(green, own, local.at[span])
+    load_green.start()
+    for r in reversed(range(span)):
+        loads[r].start()
+
+    load_green.wait()
+    greens[3 * chip] = own[0, :, :LANES]
+    greens[3 * chip + 1] = own[1, :, :LANES]
+    greens[3 * chip + 2] = join(own[0, :, LANES:], own[1, :, LANES:])
+
+    def pack(r, ch):
+        pieces = []
+        for p in range(BATCH // 2):
+            a = raw[r, ch * BATCH + 2 * p]
+            b = raw[r, ch * BATCH + 2 * p + 1]
+            pieces += [a[:, :LANES], b[:, :LANES], join(a[:, LANES:], b[:, LANES:])]
+        return pieces
+
+    def pack_chunk(ch):
+        for r in range(span):
+            for n, piece in enumerate(pack(r, ch)):
+                if r == 0:
+                    vectors[ch, walker, :, n * LANES : (n + 1) * LANES] = piece
+                else:
+                    packed[r, ch, :, n * LANES : (n + 1) * LANES] = piece
+
+    def chol_copy(ch, r):
+        return remote(packed.at[r, ch], vectors.at[ch, walker], chol_send.at[ch, r], chol_recv.at[ch, r], device(r, 0))
+
+    def pair_copy(ch, r):
+        block = vectors.at[ch, flip(chip, r) * CORES + core]
+        return remote(block, block, pair_send.at[ch, r], pair_recv.at[ch, r], partner)
+
+    def green_piece(r, e):
+        rows = pl.ds(pl.multiple_of(flip(group, e) * quarter, 16), quarter)
+        return greens.at[pl.ds(3 * flip(chip, r), 3), rows, :]
+
+    def green_copy(r, bit):
+        n = r | bit
+        return remote(green_piece(r, 0), green_piece(r, 0), green_send.at[n], green_recv.at[n], device(bit, 0))
+
+    def share_copy(r, e):
+        return remote(green_piece(r, 0), green_piece(r, 0), share_send.at[r, e], share_recv.at[r, e], device(0, e))
+
+    for r in reversed(range(span)):
+        loads[r].wait()
+    pack_chunk(0)
+    pl.semaphore_wait(barrier, len(others) + 1)
+
+    highs = [1 << b for b in reversed(range(span.bit_length() - 1))]
+    for bit in highs:
+        green_copy(0, bit).start()
+    for r in reversed(range(1, span)):
+        chol_copy(0, r).start()
+    pair_copy(0, 0).start()
+
+    def pack_rest(ch, carry):
+        pack_chunk(ch)
+        return carry
+
+    lax.fori_loop(1, chunks, pack_rest, 0)
+    total[...] = jnp.zeros_like(total)
+
+    for at, bit in enumerate(highs):
+        done = [r for r in range(span) if r % (2 * bit) == 0]
+        for r in done:
+            n = r | bit
+            green_copy(r, bit).wait_recv()
+            for low in highs[at + 1 :]:
+                green_copy(n, low).start()
+            for e in range(1, groups):
+                share_copy(n, e).start()
+
+    def send_rest(ch, carry):
+        for r in reversed(range(1, span)):
+            chol_copy(ch, r).start()
+        pair_copy(ch, 0).start()
+        return carry
+
+    lax.fori_loop(1, chunks, send_rest, 0)
+
+    for r in range(1, span):
+        for e in range(1, groups):
+            share_copy(r, e).wait_recv()
+
+    def turn(n, carry):
+        turned[n] = greens[n].T
+        return carry
+
+    lax.fori_loop(0, 3 * span, turn, 0)
+
+    def compute(ch, g):
+        left = turned[pl.ds(6 * g, 6)].reshape(2 * cell, m)
+        for n in range(3):
+            cut = slice(2 * n * LANES, 2 * (n + 1) * LANES)
+            right = vectors[ch, :, :, cut].reshape(m, 2 * LANES)
+            tmat[:, cut] = jnp.dot(left, right, preferred_element_type=jnp.float32).astype(jnp.bfloat16)
+        for k in range(2):
+            for p in range(2):
+                for at, size, step in ((0, LANES, LANES), (2 * LANES, HALF, HALF)):
+                    source = [slice(p * cell + at + step * b, p * cell + at + step * b + size) for b in range(2)]
+                    target = [slice(k * cell + at + step * a, k * cell + at + step * a + size) for a in range(2)]
+                    for a in range(2):
+                        for b in range(2):
+                            mixed[target[a], p * cell + b * LANES : p * cell + (b + 1) * LANES] = tmat[
+                                source[b], k * cell + a * LANES : k * cell + (a + 1) * LANES
+                            ]
+                    ends = [tmat[source[b], k * cell + 2 * LANES : (k + 1) * cell] for b in range(2)]
+                    for a in range(2):
+                        half = slice(a * HALF, (a + 1) * HALF)
+                        mixed[target[a], p * cell + 2 * LANES : (p + 1) * cell] = join(ends[0][:, half], ends[1][:, half])
+        whole = vectors[ch].reshape(m, 2 * cell)
+        for n in range(3):
+            sums = jnp.dot(
+                whole, mixed[:, 2 * n * LANES : 2 * (n + 1) * LANES], preferred_element_type=jnp.float32
+            )
+            total[6 * g + 2 * n] += sums[:, :LANES]
+            total[6 * g + 2 * n + 1] += sums[:, LANES:]
+
+    def rows_of(e, colour):
+        return pl.ds(pl.multiple_of(flip(group, e) * quarter + colour * part, 16), part)
+
+    def held(r, e, colour):
+        return total.at[pl.ds(3 * r, 3), rows_of(e, colour), :]
+
+    def grad_copy(s, colour, e, bit):
+        return remote(
+            outgoing.at[s, colour, e], incoming.at[s, colour, e], grad_send.at[s, colour, e], grad_recv.at[s, colour, e],
+            device(0, bit),
+        )
+
+    def first_step(s):
+        for colour, order in enumerate(orders):
+            for e in range(groups):
+                if e & order[0]:
+                    outgoing[s, colour, e] = held(s, e, colour)[...].astype(jnp.bfloat16)
+        for colour, order in enumerate(orders):
+            for e in range(groups):
+                if e & order[0]:
+                    grad_copy(s, colour, e, order[0]).start()
+
+    def chunk_step(ch, carry):
+        for r in reversed(range(1, span)):
+            chol_copy(ch, r).wait_recv()
+            pair_copy(ch, r).start()
+        for r in range(span):
+            pair_copy(ch, r).wait_recv()
+
+        def group_step(n, carry):
+            g = lax.rem(lax.div(chip, 2) + 1 + n, span // 2)
+            compute(ch, g)
+
+            @pl.when(ch == chunks - 1)
+            def _():
+                first_step(2 * g)
+                first_step(2 * g + 1)
+
+            return carry
+
+        lax.fori_loop(0, span // 2, group_step, 0)
+        return carry
+
+    lax.fori_loop(0, chunks, chunk_step, 0)
+
+    slots = [flip(chip, r) for r in reversed(range(span))]
+
+    low = lax.broadcasted_iota(jnp.int32, (8, LANES), 1) < HALF
+
+    def weigh(s, carry):
+        def rows(n, sums):
+            at = pl.ds(pl.multiple_of(n * 64, 64), 64)
+            new = []
+            for t in range(3):
+                product = greens[3 * s + t, at, :].astype(jnp.float32) * total[3 * s + t, at, :]
+                new.append(sums[t] + jnp.sum(product.reshape(8, 8, LANES), axis=0))
+            return tuple(new)
+
+        zero = jnp.zeros((8, LANES), jnp.float32)
+        sums = lax.fori_loop(0, m // 64, rows, (zero, zero, zero))
+        lines[s, 0] = sums[0] + jnp.where(low, sums[2], 0.0)
+        lines[s, 1] = sums[1] + jnp.where(low, 0.0, sums[2])
+        return carry
+
+    lax.fori_loop(0, span, weigh, 0)
+
+    def line_copy(n):
+        r, e = others[n]
+        return remote(lines.at[flip(chip, r)], arrived.at[n], line_send.at[n], line_recv.at[n], device(r, e))
+
+    for n in range(len(others)):
+        line_copy(n).start()
+
+    def grad_step(s, at):
+        for colour, order in enumerate(orders):
+            past = sum(order[:at])
+            bit = order[at]
+            ready = [e for e in range(groups) if (e & bit) and not (e & past)]
+            for e in ready:
+                grad_copy(s, colour, e, bit).wait_recv()
+                mine = e ^ bit
+                piece = held(s, mine, colour)
+                value = piece[...] + incoming[s, colour, e].astype(jnp.float32)
+                if mine == 0:
+                    piece[...] = value
+                elif mine & order[at + 1]:
+                    outgoing[s, colour, mine] = value.astype(jnp.bfloat16)
+                    grad_copy(s, colour, mine, order[at + 1]).start()
+                else:
+                    piece[...] = value
+
+    def last_copy(r):
+        return remote(last_out.at[r], last_in.at[r], last_send.at[r], last_recv.at[r], device(r, 0))
+
+    mine = pl.ds(pl.multiple_of(group * quarter, 16), quarter)
+
+    def finish(n):
+        r = span - 1 - n
+        grad_step(slots[n], len(bits) - 1)
+        if r > 0:
+            last_out[r] = total[pl.ds(3 * slots[n], 3), mine, :].astype(jnp.bfloat16)
+            last_copy(r).start()
+
+    for at in range(len(bits) - 1):
+        for n in range(span):
+            grad_step(slots[n], at)
+            if at == len(bits) - 2 and n > 1:
+                finish(n - 2)
+    for n in range(span - 2, span):
+        finish(n)
+
+    for r in range(1, span):
+        last_copy(r).wait_recv()
+    final = [total[3 * chip + t, mine, :] for t in range(3)]
+    for r in range(1, span):
+        final = [final[t] + last_in[r, t].astype(jnp.float32) for t in range(3)]
+    final = [x * gscale for x in final]
+    out[0, :, :LANES] = final[0]
+    out[1, :, :LANES] = final[1]
+    out[0, :, LANES:] = final[2][:, :HALF]
+    out[1, :, LANES:] = final[2][:, HALF:]
+
+    for n in range(len(others)):
+        line_copy(n).wait_recv()
+    sums = lines[chip]
+    for n in range(len(others)):
+        sums = sums + arrived[n]
+    energy[...] = sums
+
+    for bit in highs:
+        for r in range(span):
+            if r % (2 * bit) == 0:
+                green_copy(r, bit).wait_send()
+    for r in range(1, span):
+        for e in range(1, groups):
+            share_copy(r, e).wait_send()
+
+    def drain(ch, carry):
+        for r in range(1, span):
+            chol_copy(ch, r).wait_send()
+        for r in range(span):
+            pair_copy(ch, r).wait_send()
+        return carry
+
+    lax.fori_loop(0, chunks, drain, 0)
+    for s in range(span):
+        for colour, order in enumerate(orders):
+            for at, bit in enumerate(order):
+                for e in range(groups):
+                    if (e & bit) and not (e & sum(order[:at])):
+                        grad_copy(s, colour, e, bit).wait_send()
+    for r in range(1, span):
+        last_copy(r).wait_send()
+    for n in range(len(others)):
+        line_copy(n).wait_send()
+
+
+def fused(span, groups, gscale, chol, green):
+    kl, mb, width = chol.shape
+    wl, m, _ = green.shape
+    kept = kl // span
+    chunks = kept // BATCH
+    quarter = m // groups
+    count = span * groups - 1
+    cell = 3 * LANES
+    dma = pltpu.SemaphoreType.DMA
+    half, full = jnp.bfloat16, jnp.float32
+    return pl.pallas_call(
+        functools.partial(fused_kernel, span, groups, gscale),
+        out_shape=(
+            jax.ShapeDtypeStruct((wl, quarter, width), full),
+            jax.ShapeDtypeStruct((wl, 8, LANES), full),
+        ),
+        in_specs=[ANY, ANY],
+        out_specs=(pl.BlockSpec(memory_space=pltpu.VMEM), pl.BlockSpec(memory_space=pltpu.VMEM)),
+        scratch_shapes=[
+            pltpu.VMEM((span, kept, mb, width), half),
+            pltpu.VMEM((span, chunks, mb, 2 * cell), half),
+            pltpu.VMEM((chunks, span * CORES, mb, 2 * cell), half),
+            pltpu.VMEM((wl, m, width), half),
+            pltpu.VMEM((3 * span, m, LANES), half),
+            pltpu.VMEM((3 * span, LANES, m), half),
+            pltpu.VMEM((2 * cell, 2 * cell), half),
+            pltpu.VMEM((2 * cell, 2 * cell), half),
+            pltpu.VMEM((3 * span, m, LANES), full),
+            pltpu.VMEM((span, 2, groups, 3, quarter // 2, LANES), half),
+            pltpu.VMEM((span, 2, groups, 3, quarter // 2, LANES), half),
+            pltpu.VMEM((span, 3, quarter, LANES), half),
+            pltpu.VMEM((span, 3, quarter, LANES), half),
+            pltpu.VMEM((span, wl, 8, LANES), full),
+            pltpu.VMEM((count, wl, 8, LANES), full),
+            dma((span + 1,)),
+            dma((chunks, span)), dma((chunks, span)), dma((chunks, span)), dma((chunks, span)),
+            dma((span,)), dma((span,)), dma((span, groups)), dma((span, groups)),
+            dma((span, 2, groups)), dma((span, 2, groups)), dma((span,)), dma((span,)), dma((count,)), dma((count,)),
+        ],
+        compiler_params=pltpu.CompilerParams(collective_id=2, has_side_effects=True, vmem_limit_bytes=60 * 2**20),
+    )(chol, green)
+
+
+def fits(span, groups, chol, green):
+    kl, mb, width = chol.shape
+    wl, m, _ = green.shape
+    powers = span & (span - 1) == 0 and groups & (groups - 1) == 0
+    tiles = width == LANES + HALF and wl == 2 and mb % 16 == 0 and m % 64 == 0 and m % (groups * 32) == 0
+    return powers and tiles and span > 1 and groups > 2 and kl % (span * BATCH) == 0 and span * m * width <= 2**21
+
+
 def per_device(span, groups, chol_vectors, green):
     kl, mb, width = chol_vectors.shape
     wl, m, _ = green.shape
@@ -215,6 +588,10 @@
     escale = 1.0 / (nchol * width)
     gscale = 1.0 / nchol**0.5
     chip, group = lax.axis_index("walker") // CORES, lax.axis_index("chol")
+
+    if fits(span, groups, chol_vectors, green):
+        gradient, sums = fused(span, groups, gscale, chol_vectors, green)
+        return jnp.sum(sums, axis=(1, 2)) * escale, gradient
 
     blocks, greens = gather(span, groups, chol_vectors, green)
     chol = jnp.transpose(blocks, (1, 0, 2, 3)).reshape(kl // span, m, width)

time: 228 us -> 108 us (0.47)
  the two profiles are of different devices: /device:TPU:24 before, /device:TPU:0 now
where the time goes in v1:
time: 108 us
  Pallas kernels  102 us (94%)
  local copies, waits for them, and re-layouts  3.98 us (4%)
  other arithmetic  1.31 us (1%)
    pallas_call x1, Pallas kernels, fused(): pl.pallas_call(functools.partial(fused_kernel, span, groups, gscale), out...  102 us
    unnamed x2, local copies, waits for them, and re-layouts  3.98 us

profile of v1, /device:TPU:0, one launch (start us, length us, event | category | flops | bytes accessed | tf_op | source)
XLA Modules:
  0.0 107.5 jit_solution(9854734721977016185)
XLA Ops:
  0.6 2.2 %copy.4.green = bf16[2,768,192]{2,1,0:T(8,128)(2,1)} copy(bf16[2,768,192]{1,2,0:T(8,128)(2,1)} %param.3) | data formatting | bytes 1179648 | tf_op args[1]
  2.8 101.6 %shard_map.41 = (f32[2,192,192]{2,1,0:T(8,128)}, f32[2,8,128]{2,1,0:T(8,128)}) custom-call(bf16[64,96,192]{2,1,0:T(8,128)(2,1)} %chol.1, bf16[2,768,192]{2,1,0:T(8,128)(2,1)} %copy.4.green), custom_call_target="tpu_custom_call" | custom-call | tf_op jit(solution)/shard_map/pallas_call | solution.py:543
  104.5 0.8 reduce_sum.9
  105.3 0.5 broadcast_multiply_fusion
  105.8 1.8 %copy.6 = f32[2,192,192]{2,1,0:T(8,128)} copy(f32[2,192,192]{2,1,0:T(8,128)} %get-tuple-element.9) | data formatting | bytes 589824

commit v2 on v1

--- a/solution.py
+++ b/solution.py
@@ -226,8 +226,8 @@
 
 
 def fused_kernel(
-    span, groups, gscale, chol, green, out, energy,
-    raw, packed, vectors, own, greens, turned, tmat, mixed, total, outgoing, incoming, last_out, last_in, lines, arrived,
+    span, groups, escale, gscale, chol, green, out, energy,
+    raw, packed, vectors, greens, turned, tmat, mixed, total, outgoing, incoming, last_out, last_in, lines, arrived,
     local, chol_send, chol_recv, pair_send, pair_recv, green_send, green_recv, share_send, share_recv,
     grad_send, grad_recv, last_send, last_recv, line_send, line_recv,
 ):
@@ -254,15 +254,18 @@
     loads = [
         pltpu.make_async_copy(chol.at[pl.ds(flip(chip, r) * kept, kept)], raw.at[r], local.at[r]) for r in range(span)
     ]
-    load_green = pltpu.make_async_copy(green, own, local.at[span])
-    load_green.start()
+    greens_in = []
+    for w in range(CORES):
+        for rows, tile, at in ((slice(0, LANES), w, 0), (slice(LANES, LANES + HALF), 2, w * HALF)):
+            greens_in.append(
+                pltpu.make_async_copy(
+                    green.at[w, rows], turned.at[3 * chip + tile, at : at + rows.stop - rows.start], local.at[span + len(greens_in)]
+                )
+            )
+    for copy in greens_in:
+        copy.start()
     for r in reversed(range(span)):
         loads[r].start()
-
-    load_green.wait()
-    greens[3 * chip] = own[0, :, :LANES]
-    greens[3 * chip + 1] = own[1, :, :LANES]
-    greens[3 * chip + 2] = join(own[0, :, LANES:], own[1, :, LANES:])
 
     def pack(r, ch):
         pieces = []
@@ -288,8 +291,9 @@
         return remote(block, block, pair_send.at[ch, r], pair_recv.at[ch, r], partner)
 
     def green_piece(r, e):
-        rows = pl.ds(pl.multiple_of(flip(group, e) * quarter, 16), quarter)
-        return greens.at[pl.ds(3 * flip(chip, r), 3), rows, :]
+        size = LANES // groups
+        rows = pl.ds(pl.multiple_of(flip(group, e) * size, 16), size)
+        return turned.at[pl.ds(3 * flip(chip, r), 3), rows, :]
 
     def green_copy(r, bit):
         n = r | bit
@@ -298,6 +302,8 @@
     def share_copy(r, e):
         return remote(green_piece(r, 0), green_piece(r, 0), share_send.at[r, e], share_recv.at[r, e], device(0, e))
 
+    for copy in greens_in:
+        copy.wait()
     for r in reversed(range(span)):
         loads[r].wait()
     pack_chunk(0)
@@ -340,7 +346,7 @@
             share_copy(r, e).wait_recv()
 
     def turn(n, carry):
-        turned[n] = greens[n].T
+        greens[n] = turned[n].T
         return carry
 
     lax.fori_loop(0, 3 * span, turn, 0)
@@ -385,44 +391,24 @@
             device(0, bit),
         )
 
-    def first_step(s):
+    def ready(order, at):
+        past = sum(order[:at])
+        sent = [e for e in range(groups) if (e & order[at]) and not (e & past)]
+        return sorted(sent, key=lambda e: e == order[at])
+
+    def convert(s):
         for colour, order in enumerate(orders):
-            for e in range(groups):
-                if e & order[0]:
-                    outgoing[s, colour, e] = held(s, e, colour)[...].astype(jnp.bfloat16)
+            for e in ready(order, 0):
+                outgoing[s, colour, e] = held(s, e, colour)[...].astype(jnp.bfloat16)
+
+    def send_first(s, n):
         for colour, order in enumerate(orders):
-            for e in range(groups):
-                if e & order[0]:
-                    grad_copy(s, colour, e, order[0]).start()
-
-    def chunk_step(ch, carry):
-        for r in reversed(range(1, span)):
-            chol_copy(ch, r).wait_recv()
-            pair_copy(ch, r).start()
-        for r in range(span):
-            pair_copy(ch, r).wait_recv()
-
-        def group_step(n, carry):
-            g = lax.rem(lax.div(chip, 2) + 1 + n, span // 2)
-            compute(ch, g)
-
-            @pl.when(ch == chunks - 1)
-            def _():
-                first_step(2 * g)
-                first_step(2 * g + 1)
-
-            return carry
-
-        lax.fori_loop(0, span // 2, group_step, 0)
-        return carry
-
-    lax.fori_loop(0, chunks, chunk_step, 0)
-
-    slots = [flip(chip, r) for r in reversed(range(span))]
+            grad_copy(s, colour, ready(order, 0)[n], order[0]).start()
 
     low = lax.broadcasted_iota(jnp.int32, (8, LANES), 1) < HALF
-
-    def weigh(s, carry):
+    top = lax.broadcasted_iota(jnp.int32, (8, LANES), 0)
+
+    def weigh(s):
         def rows(n, sums):
             at = pl.ds(pl.multiple_of(n * 64, 64), 64)
             new = []
@@ -433,56 +419,93 @@
 
         zero = jnp.zeros((8, LANES), jnp.float32)
         sums = lax.fori_loop(0, m // 64, rows, (zero, zero, zero))
-        lines[s, 0] = sums[0] + jnp.where(low, sums[2], 0.0)
-        lines[s, 1] = sums[1] + jnp.where(low, 0.0, sums[2])
+        one = jnp.sum(sums[0] + jnp.where(low, sums[2], 0.0), axis=0, keepdims=True)
+        two = jnp.sum(sums[1] + jnp.where(low, 0.0, sums[2]), axis=0, keepdims=True)
+        lines[s] = jnp.where(top == 0, one, jnp.where(top == 1, two, 0.0))
+
+    def chunk_step(ch, carry):
+        for r in reversed(range(1, span)):
+            chol_copy(ch, r).wait_recv()
+            pair_copy(ch, r).start()
+        for r in range(span):
+            pair_copy(ch, r).wait_recv()
+
+        def group_step(n, carry):
+            g = lax.rem(lax.div(chip, 2) + 1 + n, span // 2)
+            compute(ch, g)
+
+            @pl.when(ch == chunks - 1)
+            def _():
+                convert(2 * g)
+                convert(2 * g + 1)
+
+            @pl.when((ch == chunks - 1) & (n == 0))
+            def _():
+                for r in (span - 1, span - 2):
+                    for i in range(groups // 2):
+                        send_first(flip(chip, r), i)
+
+            @pl.when(ch == chunks - 1)
+            def _():
+                weigh(2 * g)
+                weigh(2 * g + 1)
+
+            return carry
+
+        lax.fori_loop(0, span // 2, group_step, 0)
         return carry
 
-    lax.fori_loop(0, span, weigh, 0)
+    lax.fori_loop(0, chunks, chunk_step, 0)
+
+    slots = [flip(chip, r) for r in range(span)]
 
     def line_copy(n):
         r, e = others[n]
-        return remote(lines.at[flip(chip, r)], arrived.at[n], line_send.at[n], line_recv.at[n], device(r, e))
-
+        return remote(lines.at[slots[r]], arrived.at[n], line_send.at[n], line_recv.at[n], device(r, e))
+
+    def take(r, at, n):
+        s = slots[r]
+        for colour, order in enumerate(orders):
+            e = ready(order, at)[n]
+            grad_copy(s, colour, e, order[at]).wait_recv()
+            mine = e ^ order[at]
+            piece = held(s, mine, colour)
+            value = piece[...] + incoming[s, colour, e].astype(jnp.float32)
+            if at + 1 < len(order) and mine & order[at + 1]:
+                outgoing[s, colour, mine] = value.astype(jnp.bfloat16)
+                grad_copy(s, colour, mine, order[at + 1]).start()
+            else:
+                piece[...] = value
+
+    def last_copy(r):
+        return remote(last_out.at[r], last_in.at[r], last_send.at[r], last_recv.at[r], device(r, 0))
+
+    mine = pl.ds(pl.multiple_of(group * quarter, 16), quarter)
+
+    def settle(r):
+        take(r, 1, 0)
+        if r > 0:
+            last_out[r] = total[pl.ds(3 * slots[r], 3), mine, :].astype(jnp.bfloat16)
+            last_copy(r).start()
+
+    take(3, 0, 0)
+    take(3, 0, 1)
+    take(2, 0, 0)
+    send_first(slots[1], 0)
+    send_first(slots[1], 1)
     for n in range(len(others)):
         line_copy(n).start()
-
-    def grad_step(s, at):
-        for colour, order in enumerate(orders):
-            past = sum(order[:at])
-            bit = order[at]
-            ready = [e for e in range(groups) if (e & bit) and not (e & past)]
-            for e in ready:
-                grad_copy(s, colour, e, bit).wait_recv()
-                mine = e ^ bit
-                piece = held(s, mine, colour)
-                value = piece[...] + incoming[s, colour, e].astype(jnp.float32)
-                if mine == 0:
-                    piece[...] = value
-                elif mine & order[at + 1]:
-                    outgoing[s, colour, mine] = value.astype(jnp.bfloat16)
-                    grad_copy(s, colour, mine, order[at + 1]).start()
-                else:
-                    piece[...] = value
-
-    def last_copy(r):
-        return remote(last_out.at[r], last_in.at[r], last_send.at[r], last_recv.at[r], device(r, 0))
-
-    mine = pl.ds(pl.multiple_of(group * quarter, 16), quarter)
-
-    def finish(n):
-        r = span - 1 - n
-        grad_step(slots[n], len(bits) - 1)
-        if r > 0:
-            last_out[r] = total[pl.ds(3 * slots[n], 3), mine, :].astype(jnp.bfloat16)
-            last_copy(r).start()
-
-    for at in range(len(bits) - 1):
-        for n in range(span):
-            grad_step(slots[n], at)
-            if at == len(bits) - 2 and n > 1:
-                finish(n - 2)
-    for n in range(span - 2, span):
-        finish(n)
+    take(2, 0, 1)
+    settle(3)
+    send_first(slots[0], 0)
+    settle(2)
+    take(1, 0, 0)
+    send_first(slots[0], 1)
+    take(1, 0, 1)
+    take(0, 0, 0)
+    settle(1)
+    take(0, 0, 1)
+    settle(0)
 
     for r in range(1, span):
         last_copy(r).wait_recv()
@@ -500,7 +523,8 @@
     sums = lines[chip]
     for n in range(len(others)):
         sums = sums + arrived[n]
-    energy[...] = sums
+    for w in range(CORES):
+        energy[w] = jnp.sum(jnp.where(top == w, sums, 0.0)) * escale
 
     for bit in highs:
         for r in range(span):
@@ -530,7 +554,7 @@
         line_copy(n).wait_send()
 
 
-def fused(span, groups, gscale, chol, green):
+def fused(span, groups, escale, gscale, chol, green):
     kl, mb, width = chol.shape
     wl, m, _ = green.shape
     kept = kl // span
@@ -541,18 +565,17 @@
     dma = pltpu.SemaphoreType.DMA
     half, full = jnp.bfloat16, jnp.float32
     return pl.pallas_call(
-        functools.partial(fused_kernel, span, groups, gscale),
+        functools.partial(fused_kernel, span, groups, escale, gscale),
         out_shape=(
             jax.ShapeDtypeStruct((wl, quarter, width), full),
-            jax.ShapeDtypeStruct((wl, 8, LANES), full),
+            jax.ShapeDtypeStruct((wl,), full),
         ),
         in_specs=[ANY, ANY],
-        out_specs=(pl.BlockSpec(memory_space=pltpu.VMEM), pl.BlockSpec(memory_space=pltpu.VMEM)),
+        out_specs=(pl.BlockSpec(memory_space=pltpu.VMEM), pl.BlockSpec(memory_space=pltpu.SMEM)),
         scratch_shapes=[
             pltpu.VMEM((span, kept, mb, width), half),
             pltpu.VMEM((span, chunks, mb, 2 * cell), half),
             pltpu.VMEM((chunks, span * CORES, mb, 2 * cell), half),
-            pltpu.VMEM((wl, m, width), half),
             pltpu.VMEM((3 * span, m, LANES), half),
             pltpu.VMEM((3 * span, LANES, m), half),
             pltpu.VMEM((2 * cell, 2 * cell), half),
@@ -562,15 +585,15 @@
             pltpu.VMEM((span, 2, groups, 3, quarter // 2, LANES), half),
             pltpu.VMEM((span, 3, quarter, LANES), half),
             pltpu.VMEM((span, 3, quarter, LANES), half),
-            pltpu.VMEM((span, wl, 8, LANES), full),
-            pltpu.VMEM((count, wl, 8, LANES), full),
-            dma((span + 1,)),
+            pltpu.VMEM((span, 8, LANES), full),
+            pltpu.VMEM((count, 8, LANES), full),
+            dma((span + 2 * wl,)),
             dma((chunks, span)), dma((chunks, span)), dma((chunks, span)), dma((chunks, span)),
             dma((span,)), dma((span,)), dma((span, groups)), dma((span, groups)),
             dma((span, 2, groups)), dma((span, 2, groups)), dma((span,)), dma((span,)), dma((count,)), dma((count,)),
         ],
         compiler_params=pltpu.CompilerParams(collective_id=2, has_side_effects=True, vmem_limit_bytes=60 * 2**20),
-    )(chol, green)
+    )(chol, jnp.swapaxes(green, 1, 2))
 
 
 def fits(span, groups, chol, green):
@@ -578,7 +601,7 @@
     wl, m, _ = green.shape
     powers = span & (span - 1) == 0 and groups & (groups - 1) == 0
     tiles = width == LANES + HALF and wl == 2 and mb % 16 == 0 and m % 64 == 0 and m % (groups * 32) == 0
-    return powers and tiles and span > 1 and groups > 2 and kl % (span * BATCH) == 0 and span * m * width <= 2**21
+    return powers and tiles and span == 4 and groups == 4 and kl % (span * BATCH) == 0 and span * m * width <= 2**21
 
 
 def per_device(span, groups, chol_vectors, green):
@@ -590,8 +613,8 @@
     chip, group = lax.axis_index("walker") // CORES, lax.axis_index("chol")
 
     if fits(span, groups, chol_vectors, green):
-        gradient, sums = fused(span, groups, gscale, chol_vectors, green)
-        return jnp.sum(sums, axis=(1, 2)) * escale, gradient
+        gradient, energy = fused(span, groups, escale, gscale, chol_vectors, green)
+        return energy, gradient
 
     blocks, greens = gather(span, groups, chol_vectors, green)
     chol = jnp.transpose(blocks, (1, 0, 2, 3)).reshape(kl // span, m, width)

time: 108 us -> 99.4 us (0.920)
  Pallas kernels: 102 us -> 95.7 us
  other arithmetic: 1.31 us -> 0 us
  local copies, waits for them, and re-layouts: 3.98 us -> 2.89 us
    pallas_call x1, Pallas kernels: 102 us -> 95.7 us  [fused(): pl.pallas_call(functools.partial(fused_kernel, span, groups, escale, gsca...]
    unnamed x2, local copies, waits for them, and re-layouts: 3.98 us -> 2.89 us
where the time goes in v2:
time: 99.4 us; the launch traced here: 99.3 us
  Pallas kernels  95.7 us (96%)
  local copies, waits for them, and re-layouts  2.89 us (3%)
    pallas_call x1, Pallas kernels, fused(): pl.pallas_call(functools.partial(fused_kernel, span, groups, escale, gsca...  95.7 us
    unnamed x2, local copies, waits for them, and re-layouts  2.89 us

profile of v2, /device:TPU:0, one launch (start us, length us, event | category | flops | bytes accessed | tf_op | source)
XLA Modules:
  0.0 99.3 jit_solution(12088737282458152751)
XLA Ops:
  0.6 95.7 %shard_map.41 = (f32[2,192,192]{2,1,0:T(8,128)}, f32[2]{0:T(128)}) custom-call(bf16[64,96,192]{2,1,0:T(8,128)(2,1)} %chol.1, bf16[2,192,768]{2,1,0:T(8,128)(2,1)} %bitcast.1), custom_call_target="tpu_custom_call" | custom-call | tf_op jit(solution)/shard_map/pallas_call | solution.py:567
  96.4 1.1 %copy.6 = f32[2]{0:T(128)} copy(f32[2]{0:T(128)} %get-tuple-element.8) | data formatting | bytes 16
  97.5 1.8 %copy.7 = f32[2,192,192]{2,1,0:T(8,128)} copy(f32[2,192,192]{2,1,0:T(8,128)} %get-tuple-element.9) | data formatting | bytes 589824

commit v3 on v2

--- a/solution.py
+++ b/solution.py
@@ -246,7 +246,9 @@
     def device(r, e):
         return (flip(chip, r) * CORES + core, flip(group, e))
 
-    others = [(r, e) for r in range(span) for e in range(groups) if r + e > 0]
+    slots = [flip(chip, r) for r in range(span)]
+    turns = list(range(span - 1, 0, -1))
+    others = [(r, 0) for r in range(1, span)] + [(0, e) for e in range(1, groups)]
     barrier = pltpu.get_barrier_semaphore()
     for peer in [partner] + [device(r, e) for r, e in others]:
         pl.semaphore_signal(barrier, inc=1, device_id=peer, device_id_type=MESH)
@@ -304,15 +306,15 @@
 
     for copy in greens_in:
         copy.wait()
+    pl.semaphore_wait(barrier, len(others) + 1)
+
+    highs = [1 << b for b in reversed(range(span.bit_length() - 1))]
+    for bit in highs:
+        green_copy(0, bit).start()
     for r in reversed(range(span)):
         loads[r].wait()
     pack_chunk(0)
-    pl.semaphore_wait(barrier, len(others) + 1)
-
-    highs = [1 << b for b in reversed(range(span.bit_length() - 1))]
-    for bit in highs:
-        green_copy(0, bit).start()
-    for r in reversed(range(1, span)):
+    for r in turns:
         chol_copy(0, r).start()
     pair_copy(0, 0).start()
 
@@ -334,7 +336,7 @@
                 share_copy(n, e).start()
 
     def send_rest(ch, carry):
-        for r in reversed(range(1, span)):
+        for r in turns:
             chol_copy(ch, r).start()
         pair_copy(ch, 0).start()
         return carry
@@ -351,33 +353,31 @@
 
     lax.fori_loop(0, 3 * span, turn, 0)
 
-    def compute(ch, g):
-        left = turned[pl.ds(6 * g, 6)].reshape(2 * cell, m)
+    def compute(ch, s):
+        left = turned[pl.ds(3 * s, 3)].reshape(cell, m)
         for n in range(3):
             cut = slice(2 * n * LANES, 2 * (n + 1) * LANES)
             right = vectors[ch, :, :, cut].reshape(m, 2 * LANES)
             tmat[:, cut] = jnp.dot(left, right, preferred_element_type=jnp.float32).astype(jnp.bfloat16)
         for k in range(2):
-            for p in range(2):
-                for at, size, step in ((0, LANES, LANES), (2 * LANES, HALF, HALF)):
-                    source = [slice(p * cell + at + step * b, p * cell + at + step * b + size) for b in range(2)]
-                    target = [slice(k * cell + at + step * a, k * cell + at + step * a + size) for a in range(2)]
-                    for a in range(2):
-                        for b in range(2):
-                            mixed[target[a], p * cell + b * LANES : p * cell + (b + 1) * LANES] = tmat[
-                                source[b], k * cell + a * LANES : k * cell + (a + 1) * LANES
-                            ]
-                    ends = [tmat[source[b], k * cell + 2 * LANES : (k + 1) * cell] for b in range(2)]
-                    for a in range(2):
-                        half = slice(a * HALF, (a + 1) * HALF)
-                        mixed[target[a], p * cell + 2 * LANES : (p + 1) * cell] = join(ends[0][:, half], ends[1][:, half])
+            for at, size in ((0, LANES), (2 * LANES, HALF)):
+                source = [slice(at + size * b, at + size * (b + 1)) for b in range(2)]
+                target = [slice(k * cell + at + size * a, k * cell + at + size * (a + 1)) for a in range(2)]
+                for a in range(2):
+                    for b in range(2):
+                        mixed[target[a], b * LANES : (b + 1) * LANES] = tmat[
+                            source[b], k * cell + a * LANES : k * cell + (a + 1) * LANES
+                        ]
+                ends = [tmat[source[b], k * cell + 2 * LANES : (k + 1) * cell] for b in range(2)]
+                for a in range(2):
+                    half = slice(a * HALF, (a + 1) * HALF)
+                    mixed[target[a], 2 * LANES :] = join(ends[0][:, half], ends[1][:, half])
         whole = vectors[ch].reshape(m, 2 * cell)
-        for n in range(3):
-            sums = jnp.dot(
-                whole, mixed[:, 2 * n * LANES : 2 * (n + 1) * LANES], preferred_element_type=jnp.float32
-            )
-            total[6 * g + 2 * n] += sums[:, :LANES]
-            total[6 * g + 2 * n + 1] += sums[:, LANES:]
+        for first, size in ((0, 2), (2, 1)):
+            cut = slice(first * LANES, (first + size) * LANES)
+            sums = jnp.dot(whole, mixed[:, cut], preferred_element_type=jnp.float32)
+            for t in range(size):
+                total[3 * s + first + t] += sums[:, t * LANES : (t + 1) * LANES]
 
     def rows_of(e, colour):
         return pl.ds(pl.multiple_of(flip(group, e) * quarter + colour * part, 16), part)
@@ -406,7 +406,6 @@
             grad_copy(s, colour, ready(order, 0)[n], order[0]).start()
 
     low = lax.broadcasted_iota(jnp.int32, (8, LANES), 1) < HALF
-    top = lax.broadcasted_iota(jnp.int32, (8, LANES), 0)
 
     def weigh(s):
         def rows(n, sums):
@@ -419,49 +418,35 @@
 
         zero = jnp.zeros((8, LANES), jnp.float32)
         sums = lax.fori_loop(0, m // 64, rows, (zero, zero, zero))
-        one = jnp.sum(sums[0] + jnp.where(low, sums[2], 0.0), axis=0, keepdims=True)
-        two = jnp.sum(sums[1] + jnp.where(low, 0.0, sums[2]), axis=0, keepdims=True)
-        lines[s] = jnp.where(top == 0, one, jnp.where(top == 1, two, 0.0))
+        lines[s, :1] = jnp.sum(sums[0] + jnp.where(low, sums[2], 0.0), axis=0, keepdims=True)
+        lines[s, 1:] = jnp.sum(sums[1] + jnp.where(low, 0.0, sums[2]), axis=0, keepdims=True)
 
     def chunk_step(ch, carry):
-        for r in reversed(range(1, span)):
+        for r in turns:
             chol_copy(ch, r).wait_recv()
             pair_copy(ch, r).start()
         for r in range(span):
             pair_copy(ch, r).wait_recv()
 
-        def group_step(n, carry):
-            g = lax.rem(lax.div(chip, 2) + 1 + n, span // 2)
-            compute(ch, g)
+        for r in reversed(range(span)):
+            compute(ch, slots[r])
 
             @pl.when(ch == chunks - 1)
             def _():
-                convert(2 * g)
-                convert(2 * g + 1)
-
-            @pl.when((ch == chunks - 1) & (n == 0))
-            def _():
-                for r in (span - 1, span - 2):
-                    for i in range(groups // 2):
-                        send_first(flip(chip, r), i)
-
-            @pl.when(ch == chunks - 1)
-            def _():
-                weigh(2 * g)
-                weigh(2 * g + 1)
-
-            return carry
-
-        lax.fori_loop(0, span // 2, group_step, 0)
+                convert(slots[r])
+                if r > 1:
+                    for n in range(groups // 2):
+                        send_first(slots[r], n)
+                weigh(slots[r])
+
         return carry
 
     lax.fori_loop(0, chunks, chunk_step, 0)
-
-    slots = [flip(chip, r) for r in range(span)]
 
     def line_copy(n):
         r, e = others[n]
-        return remote(lines.at[slots[r]], arrived.at[n], line_send.at[n], line_recv.at[n], device(r, e))
+        source = lines.at[slots[r]] if e == 0 else lines.at[span]
+        return remote(source, arrived.at[n], line_send.at[n], line_recv.at[n], device(r, e))
 
     def take(r, at, n):
         s = slots[r]
@@ -493,15 +478,22 @@
     take(2, 0, 0)
     send_first(slots[1], 0)
     send_first(slots[1], 1)
-    for n in range(len(others)):
+    for n in range(span - 1):
         line_copy(n).start()
     take(2, 0, 1)
     settle(3)
     send_first(slots[0], 0)
     settle(2)
+    sums = lines[chip]
+    for n in range(span - 1):
+        line_copy(n).wait_recv()
+        sums = sums + arrived[n]
+    lines[span] = sums
     take(1, 0, 0)
     send_first(slots[0], 1)
     take(1, 0, 1)
+    for n in range(span - 1, len(others)):
+        line_copy(n).start()
     take(0, 0, 0)
     settle(1)
     take(0, 0, 1)
@@ -518,13 +510,12 @@
     out[0, :, LANES:] = final[2][:, :HALF]
     out[1, :, LANES:] = final[2][:, HALF:]
 
-    for n in range(len(others)):
+    sums = lines[span]
+    for n in range(span - 1, len(others)):
         line_copy(n).wait_recv()
-    sums = lines[chip]
-    for n in range(len(others)):
         sums = sums + arrived[n]
-    for w in range(CORES):
-        energy[w] = jnp.sum(jnp.where(top == w, sums, 0.0)) * escale
+    sums = jnp.sum(sums, axis=1, keepdims=True) * escale
+    energy[...] = join(sums[:1], sums[1:])
 
     for bit in highs:
         for r in range(span):
@@ -560,33 +551,33 @@
     kept = kl // span
     chunks = kept // BATCH
     quarter = m // groups
-    count = span * groups - 1
+    count = span + groups - 2
     cell = 3 * LANES
     dma = pltpu.SemaphoreType.DMA
     half, full = jnp.bfloat16, jnp.float32
     return pl.pallas_call(
         functools.partial(fused_kernel, span, groups, escale, gscale),
         out_shape=(
-            jax.ShapeDtypeStruct((wl, quarter, width), full),
-            jax.ShapeDtypeStruct((wl,), full),
+            pltpu.VMEM((wl, quarter, width), full),
+            pltpu.VMEM((1, wl), full),
         ),
         in_specs=[ANY, ANY],
-        out_specs=(pl.BlockSpec(memory_space=pltpu.VMEM), pl.BlockSpec(memory_space=pltpu.SMEM)),
+        out_specs=(pl.BlockSpec(memory_space=pltpu.VMEM), pl.BlockSpec(memory_space=pltpu.VMEM)),
         scratch_shapes=[
             pltpu.VMEM((span, kept, mb, width), half),
             pltpu.VMEM((span, chunks, mb, 2 * cell), half),
             pltpu.VMEM((chunks, span * CORES, mb, 2 * cell), half),
             pltpu.VMEM((3 * span, m, LANES), half),
             pltpu.VMEM((3 * span, LANES, m), half),
-            pltpu.VMEM((2 * cell, 2 * cell), half),
-            pltpu.VMEM((2 * cell, 2 * cell), half),
+            pltpu.VMEM((cell, 2 * cell), half),
+            pltpu.VMEM((2 * cell, cell), half),
             pltpu.VMEM((3 * span, m, LANES), full),
             pltpu.VMEM((span, 2, groups, 3, quarter // 2, LANES), half),
             pltpu.VMEM((span, 2, groups, 3, quarter // 2, LANES), half),
             pltpu.VMEM((span, 3, quarter, LANES), half),
             pltpu.VMEM((span, 3, quarter, LANES), half),
-            pltpu.VMEM((span, 8, LANES), full),
-            pltpu.VMEM((count, 8, LANES), full),
+            pltpu.VMEM((span + 1, wl, LANES), full),
+            pltpu.VMEM((count, wl, LANES), full),
             dma((span + 2 * wl,)),
             dma((chunks, span)), dma((chunks, span)), dma((chunks, span)), dma((chunks, span)),
             dma((span,)), dma((span,)), dma((span, groups)), dma((span, groups)),
@@ -614,7 +605,7 @@
 
     if fits(span, groups, chol_vectors, green):
         gradient, energy = fused(span, groups, escale, gscale, chol_vectors, green)
-        return energy, gradient
+        return energy[0], gradient
 
     blocks, greens = gather(span, groups, chol_vectors, green)
     chol = jnp.transpose(blocks, (1, 0, 2, 3)).reshape(kl // span, m, width)

time: 99.4 us -> 93.8 us (0.944)
  Pallas kernels: 95.7 us -> 91.8 us
  local copies, waits for them, and re-layouts: 2.89 us -> 1.26 us
    pallas_call x1, Pallas kernels: 95.7 us -> 91.8 us  [fused(): pl.pallas_call(functools.partial(fused_kernel, span, groups, escale, gsca...]
    unnamed x2, local copies, waits for them, and re-layouts: 2.89 us -> 1.26 us
where the time goes in v3:
time: 93.8 us; the launch traced here: 93.7 us
  Pallas kernels  91.8 us (98%)
  local copies, waits for them, and re-layouts  1.26 us (1%)
    pallas_call x1, Pallas kernels, fused(): pl.pallas_call(functools.partial(fused_kernel, span, groups, escale, gsca...  91.8 us

profile of v3, /device:TPU:0, one launch (start us, length us, event | category | flops | bytes accessed | tf_op | source)
XLA Modules:
  0.0 93.7 jit_solution(14198051960091328035)
XLA Ops:
  0.6 91.8 %shard_map.41 = (f32[2,192,192]{2,1,0:T(8,128)S(1)}, f32[1,2]{1,0:T(1,128)S(1)}) custom-call(bf16[64,96,192]{2,1,0:T(8,128)(2,1)} %chol.1, bf16[2,192,768]{2,1,0:T(8,128)(2,1)} %bitcast.3), custom_call_target="tpu_custom_call" | custom-call | tf_op jit(solution)/shard_map/pallas_call | solution.py:558
  92.4 0.5 copy.6
  92.9 0.7 copy.7

commit v4 on v3

--- a/solution.py
+++ b/solution.py
@@ -227,9 +227,9 @@
 
 def fused_kernel(
     span, groups, escale, gscale, chol, green, out, energy,
-    raw, packed, vectors, greens, turned, tmat, mixed, total, outgoing, incoming, last_out, last_in, lines, arrived,
+    raw, packed, vectors, greens, turned, tmat, mixed, total, outgoing, incoming, last_out, last_in, near_out, near_in, lines, arrived,
     local, chol_send, chol_recv, pair_send, pair_recv, green_send, green_recv, share_send, share_recv,
-    grad_send, grad_recv, last_send, last_recv, line_send, line_recv,
+    grad_send, grad_recv, near_send, near_recv, last_send, last_recv, line_send, line_recv,
 ):
     walker, group = lax.axis_index("walker"), lax.axis_index("chol")
     chip, core = lax.div(walker, CORES), lax.rem(walker, CORES)
@@ -239,8 +239,8 @@
     quarter = m // groups
     part = quarter // 2
     cell = 3 * LANES
-    bits = [1 << b for b in range(groups.bit_length() - 1)]
-    orders = [bits, bits[::-1]]
+    sides = [flip(group, e) for e in range(groups)]
+    near, plain = core, 1 - core
     partner = (chip * CORES + 1 - core, group)
 
     def device(r, e):
@@ -379,31 +379,27 @@
             for t in range(size):
                 total[3 * s + first + t] += sums[:, t * LANES : (t + 1) * LANES]
 
-    def rows_of(e, colour):
-        return pl.ds(pl.multiple_of(flip(group, e) * quarter + colour * part, 16), part)
-
-    def held(r, e, colour):
-        return total.at[pl.ds(3 * r, 3), rows_of(e, colour), :]
-
-    def grad_copy(s, colour, e, bit):
+    def routes(colour):
+        first = sides[1] + colour * (sides[2] - sides[1])
+        return first, sides[1] + sides[2] - first, sides[3]
+
+    def held(s, block, colour):
+        return total.at[pl.ds(3 * s, 3), pl.ds(pl.multiple_of(block * quarter + colour * part, 16), part), :]
+
+    def grad_copy(s, colour, kind):
+        first, second, _ = routes(colour)
         return remote(
-            outgoing.at[s, colour, e], incoming.at[s, colour, e], grad_send.at[s, colour, e], grad_recv.at[s, colour, e],
-            device(0, bit),
+            outgoing.at[s, colour, kind], incoming.at[s, colour, kind],
+            grad_send.at[s, colour, kind], grad_recv.at[s, colour, kind], (walker, second if kind == 2 else first),
         )
 
-    def ready(order, at):
-        past = sum(order[:at])
-        sent = [e for e in range(groups) if (e & order[at]) and not (e & past)]
-        return sorted(sent, key=lambda e: e == order[at])
-
-    def convert(s):
-        for colour, order in enumerate(orders):
-            for e in ready(order, 0):
-                outgoing[s, colour, e] = held(s, e, colour)[...].astype(jnp.bfloat16)
-
-    def send_first(s, n):
-        for colour, order in enumerate(orders):
-            grad_copy(s, colour, ready(order, 0)[n], order[0]).start()
+    def convert(s, colour):
+        first, _, both = routes(colour)
+        outgoing[s, colour, 0] = held(s, both, colour)[...].astype(jnp.bfloat16)
+        outgoing[s, colour, 1] = held(s, first, colour)[...].astype(jnp.bfloat16)
+
+    def near_copy():
+        return remote(near_out, near_in, near_send.at[0], near_recv.at[0], device(1, 0))
 
     low = lax.broadcasted_iota(jnp.int32, (8, LANES), 1) < HALF
 
@@ -422,21 +418,29 @@
         lines[s, 1:] = jnp.sum(sums[1] + jnp.where(low, 0.0, sums[2]), axis=0, keepdims=True)
 
     def chunk_step(ch, carry):
-        for r in turns:
+        for r in reversed(turns):
             chol_copy(ch, r).wait_recv()
             pair_copy(ch, r).start()
         for r in range(span):
             pair_copy(ch, r).wait_recv()
 
-        for r in reversed(range(span)):
+        for r in (3, 1, 2, 0):
             compute(ch, slots[r])
 
             @pl.when(ch == chunks - 1)
             def _():
-                convert(slots[r])
                 if r > 1:
-                    for n in range(groups // 2):
-                        send_first(slots[r], n)
+                    convert(slots[r], 0)
+                    convert(slots[r], 1)
+                    for kind in range(2):
+                        grad_copy(slots[r], 0, kind).start()
+                        grad_copy(slots[r], 1, kind).start()
+                else:
+                    convert(slots[r], plain)
+                if r == 1:
+                    for block in range(groups):
+                        near_out[block] = held(slots[1], block, near)[...].astype(jnp.bfloat16)
+                    near_copy().start()
                 weigh(slots[r])
 
         return carry
@@ -448,62 +452,73 @@
         source = lines.at[slots[r]] if e == 0 else lines.at[span]
         return remote(source, arrived.at[n], line_send.at[n], line_recv.at[n], device(r, e))
 
-    def take(r, at, n):
+    def take(r, kind, colours):
         s = slots[r]
-        for colour, order in enumerate(orders):
-            e = ready(order, at)[n]
-            grad_copy(s, colour, e, order[at]).wait_recv()
-            mine = e ^ order[at]
-            piece = held(s, mine, colour)
-            value = piece[...] + incoming[s, colour, e].astype(jnp.float32)
-            if at + 1 < len(order) and mine & order[at + 1]:
-                outgoing[s, colour, mine] = value.astype(jnp.bfloat16)
-                grad_copy(s, colour, mine, order[at + 1]).start()
+        for colour in colours:
+            grad_copy(s, colour, kind).wait_recv()
+            piece = held(s, group if kind else routes(colour)[1], colour)
+            value = piece[...] + incoming[s, colour, kind].astype(jnp.float32)
+            if kind == 0:
+                outgoing[s, colour, 2] = value.astype(jnp.bfloat16)
+                grad_copy(s, colour, 2).start()
             else:
                 piece[...] = value
 
-    def last_copy(r):
-        return remote(last_out.at[r], last_in.at[r], last_send.at[r], last_recv.at[r], device(r, 0))
+    def send_first(r, colour):
+        for kind in range(2):
+            grad_copy(slots[r], colour, kind).start()
 
     mine = pl.ds(pl.multiple_of(group * quarter, 16), quarter)
 
-    def settle(r):
-        take(r, 1, 0)
-        if r > 0:
-            last_out[r] = total[pl.ds(3 * slots[r], 3), mine, :].astype(jnp.bfloat16)
-            last_copy(r).start()
-
-    take(3, 0, 0)
-    take(3, 0, 1)
-    take(2, 0, 0)
-    send_first(slots[1], 0)
-    send_first(slots[1], 1)
+    def last_copy(r, colour):
+        return remote(
+            last_out.at[r, colour], last_in.at[r, colour], last_send.at[r, colour], last_recv.at[r, colour], device(r, 0)
+        )
+
+    def settle(r, colours):
+        for colour in colours:
+            take(r, 2, (colour,))
+            last_out[r, colour] = held(slots[r], group, colour)[...].astype(jnp.bfloat16)
+            last_copy(r, colour).start()
+
+    take(3, 0, (0, 1))
+    take(3, 1, (0, 1))
+    take(2, 0, (0, 1))
+    send_first(1, plain)
     for n in range(span - 1):
         line_copy(n).start()
-    take(2, 0, 1)
-    settle(3)
-    send_first(slots[0], 0)
-    settle(2)
+    take(2, 1, (0, 1))
+    settle(3, (0, 1))
+    send_first(0, plain)
+    settle(2, (0, 1))
     sums = lines[chip]
     for n in range(span - 1):
         line_copy(n).wait_recv()
         sums = sums + arrived[n]
     lines[span] = sums
-    take(1, 0, 0)
-    send_first(slots[0], 1)
-    take(1, 0, 1)
+    take(1, 0, (plain,))
+    near_copy().wait_recv()
+    for block in range(groups):
+        piece = held(chip, block, near)
+        piece[...] = piece[...] + near_in[block].astype(jnp.float32)
+    convert(chip, near)
+    send_first(0, near)
+    take(1, 1, (plain,))
     for n in range(span - 1, len(others)):
         line_copy(n).start()
-    take(0, 0, 0)
-    settle(1)
-    take(0, 0, 1)
-    settle(0)
-
-    for r in range(1, span):
-        last_copy(r).wait_recv()
+    take(0, 0, (plain,))
+    take(0, 1, (plain,))
+    settle(1, (plain,))
+    take(0, 0, (near,))
+    take(0, 1, (near,))
+    take(0, 2, (plain, near))
+
+    for r in range(span - 1, 0, -1):
+        for colour in (plain,) if r == 1 else (0, 1):
+            last_copy(r, colour).wait_recv()
+            piece = held(chip, group, colour)
+            piece[...] = piece[...] + last_in[r, colour].astype(jnp.float32)
     final = [total[3 * chip + t, mine, :] for t in range(3)]
-    for r in range(1, span):
-        final = [final[t] + last_in[r, t].astype(jnp.float32) for t in range(3)]
     final = [x * gscale for x in final]
     out[0, :, :LANES] = final[0]
     out[1, :, :LANES] = final[1]
@@ -533,14 +548,14 @@
         return carry
 
     lax.fori_loop(0, chunks, drain, 0)
-    for s in range(span):
-        for colour, order in enumerate(orders):
-            for at, bit in enumerate(order):
-                for e in range(groups):
-                    if (e & bit) and not (e & sum(order[:at])):
-                        grad_copy(s, colour, e, bit).wait_send()
+    for r in range(span):
+        for colour in (plain,) if r == 1 else (0, 1):
+            for kind in range(3):
+                grad_copy(slots[r], colour, kind).wait_send()
+    near_copy().wait_send()
     for r in range(1, span):
-        last_copy(r).wait_send()
+        for colour in (plain,) if r == 1 else (0, 1):
+            last_copy(r, colour).wait_send()
     for n in range(len(others)):
         line_copy(n).wait_send()
 
@@ -572,16 +587,18 @@
             pltpu.VMEM((cell, 2 * cell), half),
             pltpu.VMEM((2 * cell, cell), half),
             pltpu.VMEM((3 * span, m, LANES), full),
-            pltpu.VMEM((span, 2, groups, 3, quarter // 2, LANES), half),
-            pltpu.VMEM((span, 2, groups, 3, quarter // 2, LANES), half),
-            pltpu.VMEM((span, 3, quarter, LANES), half),
-            pltpu.VMEM((span, 3, quarter, LANES), half),
+            pltpu.VMEM((span, 2, 3, 3, quarter // 2, LANES), half),
+            pltpu.VMEM((span, 2, 3, 3, quarter // 2, LANES), half),
+            pltpu.VMEM((span, 2, 3, quarter // 2, LANES), half),
+            pltpu.VMEM((span, 2, 3, quarter // 2, LANES), half),
+            pltpu.VMEM((groups, 3, quarter // 2, LANES), half),
+            pltpu.VMEM((groups, 3, quarter // 2, LANES), half),
             pltpu.VMEM((span + 1, wl, LANES), full),
             pltpu.VMEM((count, wl, LANES), full),
             dma((span + 2 * wl,)),
             dma((chunks, span)), dma((chunks, span)), dma((chunks, span)), dma((chunks, span)),
             dma((span,)), dma((span,)), dma((span, groups)), dma((span, groups)),
-            dma((span, 2, groups)), dma((span, 2, groups)), dma((span,)), dma((span,)), dma((count,)), dma((count,)),
+            dma((span, 2, 3)), dma((span, 2, 3)), dma((1,)), dma((1,)), dma((span, 2)), dma((span, 2)), dma((count,)), dma((count,)),
         ],
         compiler_params=pltpu.CompilerParams(collective_id=2, has_side_effects=True, vmem_limit_bytes=60 * 2**20),
     )(chol, jnp.swapaxes(green, 1, 2))

time: 93.8 us -> 93.2 us (level)
  no operation moved by 1% of the time
where the time goes in v4:
time: 93.2 us; the launch traced here: 93.1 us
  Pallas kernels  91.2 us (98%)
  local copies, waits for them, and re-layouts  1.26 us (1%)
    pallas_call x1, Pallas kernels, fused(): pl.pallas_call(functools.partial(fused_kernel, span, groups, escale, gsca...  91.2 us

profile of v4, /device:TPU:0, one launch (start us, length us, event | category | flops | bytes accessed | tf_op | source)
XLA Modules:
  0.0 93.1 jit_solution(14107521681959050017)
XLA Ops:
  0.6 91.2 %shard_map.41 = (f32[2,192,192]{2,1,0:T(8,128)S(1)}, f32[1,2]{1,0:T(1,128)S(1)}) custom-call(bf16[64,96,192]{2,1,0:T(8,128)(2,1)} %chol.1, bf16[2,192,768]{2,1,0:T(8,128)(2,1)} %bitcast.3), custom_call_target="tpu_custom_call" | custom-call | tf_op jit(solution)/shard_map/pallas_call | solution.py:573
  91.8 0.5 copy.6
  92.3 0.7 copy.7
